TPU v7x, 256 devices: a whole 4x4x8 slice. The times are simulated.
256 devices in a mesh: cells: 32 (over y, z), bins: 8 (over x, core).
Axes of the slice: x: 4, y: 4, z: 8, core: 2. Of those that a mesh axis runs over, the one named last changes fastest.
Arguments:
- snapshots: bfloat16 [8, 262144, 512], P('bins', 'cells'), may hold values from -150 to 150
- training: int32 [262144], P('cells'), may hold values 0 or 1
- doppler: int32 [8, 128], P('bins'), may hold values from 0 to 1023
Outputs:
- filtered: bfloat16 [8, 256, 262144], P('bins', None, 'cells')
All inputs are finite; a program needn't handle non-finite values. No bound on the sum of `training` on one device may be relied on, other than what follows from the above.
Results may differ from a plain program's by a relative error of at most 0.003.
The roundings to bfloat16 on the way count: a program that leaves them out, or rounds other values in their place, can miss the bound.
Values sent between devices are 32-bit elements; how exact they have to be, the bound alone decides.
No kernel may reach another device: no remote copies, remote signals or barrier semaphores. Data moves between devices by JAX's collectives and lax.ppermute only.
A program may use at most 64 MiB of HBM per device.

v0:
```python
import functools

import jax
import jax.numpy as jnp
from jax import lax
from jax.experimental import pallas as pl
from jax.experimental.pallas import tpu as pltpu
from jax.sharding import PartitionSpec as P

CHANNELS = 16
PULSES = 16
NDOPP = 1024
LANES = 128
GRAM_CELLS = 1024
FILTER_CELLS = 1024

load_ratio = 0.5
look_freq = 0.125

bf16 = jnp.bfloat16
f32 = jnp.float32


def dot(a, b):
    return jnp.dot(a, b, preferred_element_type=f32)


def gram_body(x_ref, keep_ref, out_ref, acc_ref):
    step = pl.program_id(0)
    half = x_ref.shape[1] // 2

    @pl.when(step == 0)
    def _():
        acc_ref[...] = jnp.zeros_like(acc_ref)

    x = x_ref[...]
    kept = x.T * keep_ref[...].astype(f32).astype(bf16)
    by_real = dot(kept, x[:, :half])
    by_imag = dot(kept[half:], x[:, half:])
    acc_ref[:half] += by_real[:half] + by_imag
    acc_ref[half:] += by_real[half:]

    @pl.when(step == pl.num_programs(0) - 1)
    def _():
        real = acc_ref[:half]
        cross = acc_ref[half:]
        imag = cross - cross.T
        rows = lax.broadcasted_iota(jnp.int32, (half, half), 0)
        cols = lax.broadcasted_iota(jnp.int32, (half, half), 1)
        packed = jnp.where(rows <= cols, real, imag)
        trace = jnp.sum(jnp.where(rows == cols, real, 0.0), keepdims=True)
        parts = half // 8
        span = out_ref.shape[0] // parts
        for part in range(parts):
            lines = packed[8 * part : 8 * part + 8]
            for block in range(half // LANES):
                out_ref[span * part + 8 * block : span * part + 8 * block + 8] = lines[
                    :, LANES * block : LANES * block + LANES
                ]
            out_ref[span * part + span - 1 : span * part + span] = jnp.broadcast_to(trace, (1, LANES))


def local_gram(snaps, keep):
    cells, width = snaps.shape
    half = width // 2
    span = 8 * half // LANES + 1
    return pl.pallas_call(
        gram_body,
        grid=(cells // GRAM_CELLS,),
        in_specs=[
            pl.BlockSpec((GRAM_CELLS, width), lambda i: (i, 0)),
            pl.BlockSpec((1, GRAM_CELLS), lambda i: (0, i)),
        ],
        out_specs=pl.BlockSpec((half // 8 * span, LANES), lambda i: (0, 0)),
        out_shape=jax.ShapeDtypeStruct((half // 8 * span, LANES), f32),
        scratch_shapes=[pltpu.VMEM((width, half), f32)],
        name="gram",
    )(snaps, keep)


def halves(x):
    top = x.astype(bf16)
    return top, (x - top.astype(f32)).astype(bf16)


def three(ah, al, bh, bl):
    return dot(jnp.concatenate([ah, ah, al], 1), jnp.concatenate([bh, bl, bh], 0))


def solve_body(gathered_ref, power_ref, sr_ref, si_ref, out_ref, ar, ai, er, ei, xr, xi):
    n = ar.shape[0]
    lines = gathered_ref[...].reshape(n // 8, n // LANES, 8, LANES)
    p = jnp.concatenate([lines[:, b].reshape(n, LANES) for b in range(n // LANES)], 1)
    rows = lax.broadcasted_iota(jnp.int32, (n, n), 0)
    cols = lax.broadcasted_iota(jnp.int32, (n, n), 1)
    eye = rows == cols
    pt = p.T
    re = jnp.where(rows <= cols, p, pt)
    im = jnp.where(rows > cols, p, jnp.where(rows < cols, -pt, 0.0))
    squares = 2.0 * p * p - jnp.where(eye, p * p, 0.0)
    low = load_ratio * power_ref[0:1, 0:1]
    high = jnp.sqrt(jnp.sum(squares, keepdims=True)) + low
    alpha = 2.0 / (low + high)
    rho = ((high - low) / (high + low))[0, 0]
    full = jnp.where(eye, re + low, re)
    ar[...] = full
    ai[...] = im
    er[...] = jnp.where(eye, 1.0, 0.0) - alpha * full
    ei[...] = -alpha * im
    xr[...] = alpha * jnp.where(eye, 1.0, 0.0)
    xi[...] = jnp.zeros_like(im)

    def step(exact, rho):
        e_r, e_i, x_r, x_i = er[...], ei[...], xr[...], xi[...]
        if exact:
            (rh, rl), (ih, il) = halves(e_r), halves(e_i)
            (xh, xl), (yh, yl) = halves(x_r), halves(x_i)
            top = jnp.concatenate([rh, ih, xh, yh], 1)
            rest = jnp.concatenate([rl, il, xl, yl], 1)
            by_real = three(rh, rl, top, rest)
            by_imag = three(ih, il, top, rest)
        else:
            both = jnp.concatenate([v.astype(bf16) for v in (e_r, e_i, x_r, x_i)], 1)
            by_real = dot(both[:, :n], both)
            by_imag = dot(both[:, n : 2 * n], both)
        mu = 2.0 / (2.0 - rho * rho)
        er[...] = mu * (by_real[:, :n] - by_imag[:, n : 2 * n]) + jnp.where(eye, 1.0 - mu, 0.0)
        ei[...] = mu * (by_real[:, n : 2 * n] + by_imag[:, :n])
        xr[...] = mu * (x_r + by_real[:, 2 * n : 3 * n] - by_imag[:, 3 * n :])
        xi[...] = mu * (x_i + by_real[:, 3 * n :] + by_imag[:, 2 * n : 3 * n])
        return rho * rho * mu * 0.5

    rho = lax.while_loop(lambda r: r > 0.5, functools.partial(step, True), rho)
    lax.while_loop(lambda r: r > 1e-3, functools.partial(step, False), rho)
    s_r, s_i = sr_ref[...], si_ref[...]
    (xh, xl), (yh, yl) = halves(xr[...]), halves(xi[...])
    top = jnp.concatenate([jnp.concatenate([xh, -yh], 1), jnp.concatenate([yh, xh], 1)], 0)
    rest = jnp.concatenate([jnp.concatenate([xl, -yl], 1), jnp.concatenate([yl, xl], 1)], 0)

    def applied(v_r, v_i):
        (rh, rl), (ih, il) = halves(v_r), halves(v_i)
        return three(jnp.concatenate([rh, ih], 1), jnp.concatenate([rl, il], 1), top, rest)

    w = applied(s_r, s_i)
    a = jnp.concatenate(
        [jnp.concatenate([ar[...], -ai[...]], 1), jnp.concatenate([ai[...], ar[...]], 1)], 0
    )
    back = jnp.dot(w, a, precision=lax.Precision.HIGHEST, preferred_element_type=f32)
    w = w + applied(s_r - back[:, :n], s_i - back[:, n:])
    w_r, w_i = w[:, :n], w[:, n:]
    gain = jnp.sum(s_r * w_r + s_i * w_i, axis=1, keepdims=True)
    t_r = (w_r / gain).astype(bf16)
    t_i = (w_i / gain).astype(bf16)
    m = s_r.shape[0]
    out_ref[:m, :n] = t_r
    out_ref[:m, n:] = t_i
    out_ref[m:, :n] = -t_i
    out_ref[m:, n:] = t_r


def solve(gathered, noise, steer_real, steer_imag):
    m, n = steer_real.shape
    return pl.pallas_call(
        solve_body,
        out_shape=jax.ShapeDtypeStruct((2 * m, 2 * n), bf16),
        scratch_shapes=[pltpu.VMEM((n, n), f32)] * 6,
        name="solve",
    )(gathered, noise, steer_real, steer_imag)


def filter_body(taps_ref, x_ref, out_ref):
    out_ref[...] = lax.dot_general(
        taps_ref[...], x_ref[...], (((1,), (1,)), ((), ())), preferred_element_type=f32
    ).astype(bf16)


def filtered(taps, snaps):
    cells, width = snaps.shape
    return pl.pallas_call(
        filter_body,
        grid=(cells // FILTER_CELLS,),
        in_specs=[
            pl.BlockSpec(taps.shape, lambda i: (0, 0)),
            pl.BlockSpec((FILTER_CELLS, width), lambda i: (i, 0)),
        ],
        out_specs=pl.BlockSpec((taps.shape[0], FILTER_CELLS), lambda i: (0, i)),
        out_shape=jax.ShapeDtypeStruct((taps.shape[0], cells), bf16),
        name="filter",
    )(taps, snaps)


def steering(doppler, chans, pulses):
    index = jnp.arange(chans * pulses)
    chan = (index // pulses).astype(f32)
    pulse = (index % pulses).astype(f32)
    freq = doppler.astype(f32) / NDOPP - 0.5
    phase = 2.0 * jnp.pi * (look_freq * chan[None, :] + pulse[None, :] * freq[:, None])
    scale = jnp.sqrt(f32(chans * pulses))
    return jnp.cos(phase) / scale, jnp.sin(phase) / scale


def exchange(x, axis):
    return lax.all_to_all(x, axis, split_axis=0, concat_axis=0, tiled=True)


def sum_of_few(x, axis):
    size = lax.axis_size(axis)
    stride = 1
    while stride < size:
        x = x + lax.ppermute(x, axis, [(i, i ^ stride) for i in range(size)])
        stride *= 2
    return x


def per_device(snapshots, training, doppler):
    snaps = snapshots[0]
    cells, width = snaps.shape
    half = width // 2
    parts = lax.axis_size("cells")
    sums = local_gram(snaps, training.reshape(1, cells))
    own = exchange(sums.reshape(parts, 1, -1), "cells").sum(axis=0)
    count = 8 * half
    lines = own[0, :count].reshape(-1, LANES)
    trace = own[:, count:]
    gathered = exchange(jnp.broadcast_to(lines, (parts, *lines.shape)), "cells")
    power = sum_of_few(trace, "bins")
    noise = power / (lax.axis_size("bins") * half)
    steer_real, steer_imag = steering(doppler[0], CHANNELS, PULSES)
    taps = solve(gathered.reshape(-1, LANES), noise, steer_real, steer_imag)
    return filtered(taps, snaps)[None]


def solution(mesh):
    in_specs = (P("bins", "cells", None), P("cells"), P("bins", None))
    out_specs = P("bins", None, "cells")
    return jax.shard_map(
        per_device, mesh=mesh, in_specs=in_specs, out_specs=out_specs, check_vma=False
    )
```

profile of v0, /device:TPU:38, one launch (start us, length us, event | category | flops | bytes accessed | tf_op | source)
XLA Modules:
  0.0 69.3 jit_solution(2805695203212122883)
XLA Ops:
  0.0 0.0 copy-start.1
  0.0 9.2 %gram.1 = f32[544,128]{1,0:T(8,128)} custom-call(bf16[8192,512]{1,0:T(8,128)(2,1)} %bitcast.8, s32[1,8192]{1,0:T(1,128)} %bitcast.12), custom_call_target="tpu_custom_call" | custom-call | tf_op jit(solution)/shard_map/gram/pallas_call | solution.py:67
  9.2 11.4 %all-to-all-start = ((f32[32,1,2176]{2,1,0:T(1,128)}), f32[32,1,2176]{2,1,0:T(1,128)S(1)}, u32[]{:S(2)}, u32[]{:S(2)}) async-start(f32[32,1,2176]{2,1,0:T(1,128)} %bitcast.10), calls=%async_computation | async-start | bytes 557056 | tf_op jit(solution)/shard_map/all_to_all | solution.py:203
  20.6 0.0 copy-done.1
  20.6 12.6 %all-to-all-done = f32[32,1,2176]{2,1,0:T(1,128)S(1)} async-done(((f32[32,1,2176]{2,1,0:T(1,128)}), f32[32,1,2176]{2,1,0:T(1,128)S(1)}, u32[]{:S(2)}, u32[]{:S(2)}) %all-to-all-start) | async-done | bytes 278560 | tf_op jit(solution)/shard_map/all_to_all | solution.py:203
  33.2 0.2 reduce_sum.11
  33.4 0.1 collective-permute-start
  33.5 0.7 %broadcast_in_dim.4 = f32[32,16,128]{2,1,0:T(8,128)} broadcast(f32[16,128]{1,0:T(8,128)S(1)} %bitcast.13), dimensions={1,2} | broadcast | bytes 270336 | tf_op jit(solution)/shard_map/broadcast_in_dim | solution.py:225
  34.2 4.6 %all-to-all-start.1 = ((f32[32,16,128]{2,1,0:T(8,128)}), f32[32,16,128]{2,1,0:T(8,128)S(1)}, u32[]{:S(2)}, u32[]{:S(2)}) async-start(f32[32,16,128]{2,1,0:T(8,128)} %broadcast_in_dim.4), calls=%async_computation.1 | async-start | bytes 524288 | tf_op jit(solution)/shard_map/all_to_all | solution.py:203
  38.9 0.0 collective-permute-done
  38.9 0.9 %collective-permute-start.1 = (f32[1,128]{1,0:T(1,128)S(1)}, f32[1,128]{1,0:T(1,128)S(1)}, u32[]{:S(2)}, u32[]{:S(2)}) collective-permute-start(f32[1,128]{1,0:T(1,128)S(1)} %slice_add_fusion), channel_id=1, source_target_pairs={{0,2},{1,3},{2,0},{3,1},{4,6},{5,7},{6,4},{7,5},{8,10},{9,11},{10,... | collective-permute-start | bytes 1544 | tf_op jit(solution)/shard_map/ppermute | solution.py:210
  39.8 2.7 %collective-permute-done.1 = f32[1,128]{1,0:T(1,128)S(1)} collective-permute-done((f32[1,128]{1,0:T(1,128)S(1)}, f32[1,128]{1,0:T(1,128)S(1)}, u32[]{:S(2)}, u32[]{:S(2)}) %collective-permute-start.1) | collective-permute-done | bytes 544 | tf_op jit(solution)/shard_map/ppermute | solution.py:210
  42.5 1.4 %collective-permute-start.2 = (f32[1,128]{1,0:T(1,128)S(1)}, f32[1,128]{1,0:T(1,128)S(1)}, u32[]{:S(2)}, u32[]{:S(2)}) collective-permute-start(f32[1,128]{1,0:T(1,128)S(1)} %add.39), channel_id=1, source_target_pairs={{0,4},{1,5},{2,6},{3,7},{4,0},{5,1},{6,2},{7,3},{8,12},{9,13},{10,... | collective-permute-start | bytes 1544 | tf_op jit(solution)/shard_map/ppermute | solution.py:210
  43.9 1.3 %sine_multiply_fusion = (f32[128,256]{1,0:T(8,128)}, f32[128,256]{1,0:T(8,128)}) fusion(f32[128]{0:T(128)S(1)} %add_bitcast_fusion, f32[256]{0:T(256)S(1)} %fusion.2, f32[256]{0:T(256)S(1)} %fusion.4), kind=kLoop, calls=%fused_computation | loop fusion | flops 163840 | bytes 264704 | tf_op jit(solution)/shard_map/div | solution.py:199
  45.2 2.4 %collective-permute-done.2 = f32[1,128]{1,0:T(1,128)S(1)} collective-permute-done((f32[1,128]{1,0:T(1,128)S(1)}, f32[1,128]{1,0:T(1,128)S(1)}, u32[]{:S(2)}, u32[]{:S(2)}) %collective-permute-start.2) | collective-permute-done | bytes 544 | tf_op jit(solution)/shard_map/ppermute | solution.py:210
  47.6 0.5 add_multiply_fusion.1.power_ref
  48.1 3.6 %all-to-all-done.1 = f32[32,16,128]{2,1,0:T(8,128)S(1)} async-done(((f32[32,16,128]{2,1,0:T(8,128)}), f32[32,16,128]{2,1,0:T(8,128)S(1)}, u32[]{:S(2)}, u32[]{:S(2)}) %all-to-all-start.1) | async-done | bytes 262176 | tf_op jit(solution)/shard_map/all_to_all | solution.py:203
  51.8 0.0 copy-start
  51.8 0.7 %copy-done = f32[32,16,128]{2,1,0:T(8,128)} copy-done((f32[32,16,128]{2,1,0:T(8,128)}, f32[32,16,128]{2,1,0:T(8,128)S(1)}, u32[]{:S(2)}) %copy-start) | copy-done | bytes 262168
  52.5 7.8 %solve.1.taps_ref = bf16[256,512]{1,0:T(8,128)(2,1)} custom-call(f32[512,128]{1,0:T(8,128)} %bitcast.11, f32[1,128]{1,0:T(1,128)} %add_multiply_fusion.1.power_ref, f32[128,256]{1,0:T(8,128)} %get-tuple-element.6.sr_ref, f32[128,256]{1,0:T(8,128)} %get-tuple-element.5.si_ref), custom_call_target="tpu_custom_call" | custom-call | tf_op jit(solution)/shard_map/solve/pallas_call | solution.py:163
  60.3 9.0 %filter.1 = bf16[256,8192]{1,0:T(8,128)(2,1)} custom-call(bf16[256,512]{1,0:T(8,128)(2,1)} %solve.1.taps_ref, bf16[8192,512]{1,0:T(8,128)(2,1)} %bitcast.9), custom_call_target="tpu_custom_call" | custom-call | tf_op jit(solution)/shard_map/filter/pallas_call | solution.py:179
  (8 shorter events, 0.0 us)
Async XLA Ops:
  0.0 20.6 %copy-start.1 = (s32[1,128]{1,0:T(1,128)S(1)}, s32[1,128]{1,0:T(1,128)}, u32[]{:S(2)}) copy-start(s32[1,128]{1,0:T(1,128)} %param.5) | copy-start | bytes 1540
  9.2 24.0 %all-to-all-start = ((f32[32,1,2176]{2,1,0:T(1,128)}), f32[32,1,2176]{2,1,0:T(1,128)S(1)}, u32[]{:S(2)}, u32[]{:S(2)}) async-start(f32[32,1,2176]{2,1,0:T(1,128)} %bitcast.10), calls=%async_computation | async-start | bytes 557056 | tf_op jit(solution)/shard_map/all_to_all | solution.py:203
  33.4 5.4 %collective-permute-start = (f32[1,128]{1,0:T(1,128)S(1)}, f32[1,128]{1,0:T(1,128)S(1)}, u32[]{:S(2)}, u32[]{:S(2)}) collective-permute-start(f32[1,128]{1,0:T(1,128)S(1)} %slice.9), channel_id=1, source_target_pairs={{0,1},{1,0},{2,3},{3,2},{4,5},{5,4},{6,7},{7,6},{8,9},{9,8},{10,11... | collective-permute-start | bytes 1544 | tf_op jit(solution)/shard_map/ppermute | solution.py:210
  34.2 17.5 %all-to-all-start.1 = ((f32[32,16,128]{2,1,0:T(8,128)}), f32[32,16,128]{2,1,0:T(8,128)S(1)}, u32[]{:S(2)}, u32[]{:S(2)}) async-start(f32[32,16,128]{2,1,0:T(8,128)} %broadcast_in_dim.4), calls=%async_computation.1 | async-start | bytes 524288 | tf_op jit(solution)/shard_map/all_to_all | solution.py:203
  38.9 3.7 %collective-permute-start.1 = (f32[1,128]{1,0:T(1,128)S(1)}, f32[1,128]{1,0:T(1,128)S(1)}, u32[]{:S(2)}, u32[]{:S(2)}) collective-permute-start(f32[1,128]{1,0:T(1,128)S(1)} %slice_add_fusion), channel_id=1, source_target_pairs={{0,2},{1,3},{2,0},{3,1},{4,6},{5,7},{6,4},{7,5},{8,10},{9,11},{10,... | collective-permute-start | bytes 1544 | tf_op jit(solution)/shard_map/ppermute | solution.py:210
  42.5 5.1 %collective-permute-start.2 = (f32[1,128]{1,0:T(1,128)S(1)}, f32[1,128]{1,0:T(1,128)S(1)}, u32[]{:S(2)}, u32[]{:S(2)}) collective-permute-start(f32[1,128]{1,0:T(1,128)S(1)} %add.39), channel_id=1, source_target_pairs={{0,4},{1,5},{2,6},{3,7},{4,0},{5,1},{6,2},{7,3},{8,12},{9,13},{10,... | collective-permute-start | bytes 1544 | tf_op jit(solution)/shard_map/ppermute | solution.py:210
  51.8 0.7 %copy-start = (f32[32,16,128]{2,1,0:T(8,128)}, f32[32,16,128]{2,1,0:T(8,128)S(1)}, u32[]{:S(2)}) copy-start(f32[32,16,128]{2,1,0:T(8,128)S(1)} %all-to-all-done.1) | copy-start | bytes 786436
where the time goes:
time: 70.4 us; the launch traced here: 69.3 us
  Pallas kernels  26 us (37%)
  waiting for transfers between devices  21.4 us (30%)
  starting transfers between devices  18.4 us (26%)
  other arithmetic  1.97 us (3%)
  local copies, waits for them, and re-layouts  1.44 us (2%)
    all_to_all x2, waiting for transfers between devices, exchange(): return lax.all_to_all(x, axis, split_axis=0, concat_axis=0, tiled=True)  16.2 us
    all_to_all x2, starting transfers between devices, exchange(): return lax.all_to_all(x, axis, split_axis=0, concat_axis=0, tiled=True)  16 us
    pallas_call x1, Pallas kernels, local_gram(): pl.pallas_call(gram_body, grid=(cells // GRAM_CELLS,), in_specs=[pl.Block...  9.23 us
    pallas_call x1, Pallas kernels, filtered(): pl.pallas_call(filter_body, grid=(cells // FILTER_CELLS,), in_specs=[pl.B...  9.03 us
    pallas_call x1, Pallas kernels, solve(): pl.pallas_call(solve_body, out_shape=jax.ShapeDtypeStruct((2 * m, 2 * n),...  7.78 us
    ppermute x3, waiting for transfers between devices, sum_of_few(): x = x + lax.ppermute(x, axis, [(i, i ^ stride) for i in range(size)])  5.15 us
    ppermute x3, starting transfers between devices, sum_of_few(): x = x + lax.ppermute(x, axis, [(i, i ^ stride) for i in range(size)])  2.42 us
  transfers between devices with their start and end apart: 5, of which 4 were waited for; matrix products, arithmetic and copies ran while one was open for 4% of the time, Pallas kernels for 0%

commit v1 on v0

--- a/solution.py
+++ b/solution.py
@@ -11,8 +11,9 @@
 PULSES = 16
 NDOPP = 1024
 LANES = 128
-GRAM_CELLS = 1024
-FILTER_CELLS = 1024
+GRAM_CELLS = 2048
+GRAM_AHEAD = 4
+FILTER_CELLS = 2048
 
 load_ratio = 0.5
 look_freq = 0.125
@@ -25,39 +26,56 @@
     return jnp.dot(a, b, preferred_element_type=f32)
 
 
-def gram_body(x_ref, keep_ref, out_ref, acc_ref):
-    step = pl.program_id(0)
-    half = x_ref.shape[1] // 2
-
-    @pl.when(step == 0)
-    def _():
-        acc_ref[...] = jnp.zeros_like(acc_ref)
-
-    x = x_ref[...]
-    kept = x.T * keep_ref[...].astype(f32).astype(bf16)
-    by_real = dot(kept, x[:, :half])
-    by_imag = dot(kept[half:], x[:, half:])
-    acc_ref[:half] += by_real[:half] + by_imag
-    acc_ref[half:] += by_real[half:]
-
-    @pl.when(step == pl.num_programs(0) - 1)
-    def _():
-        real = acc_ref[:half]
-        cross = acc_ref[half:]
-        imag = cross - cross.T
-        rows = lax.broadcasted_iota(jnp.int32, (half, half), 0)
-        cols = lax.broadcasted_iota(jnp.int32, (half, half), 1)
-        packed = jnp.where(rows <= cols, real, imag)
-        trace = jnp.sum(jnp.where(rows == cols, real, 0.0), keepdims=True)
-        parts = half // 8
-        span = out_ref.shape[0] // parts
-        for part in range(parts):
-            lines = packed[8 * part : 8 * part + 8]
-            for block in range(half // LANES):
-                out_ref[span * part + 8 * block : span * part + 8 * block + 8] = lines[
-                    :, LANES * block : LANES * block + LANES
-                ]
-            out_ref[span * part + span - 1 : span * part + span] = jnp.broadcast_to(trace, (1, LANES))
+def gram_body(x_hbm, keep_hbm, out_ref, x_ref, keep_ref, acc_ref, sems):
+    cells, width = x_ref.shape
+    half = width // 2
+    steps = cells // GRAM_CELLS
+
+    def copy(step):
+        rows = pl.ds(pl.multiple_of(step * GRAM_CELLS, GRAM_CELLS), GRAM_CELLS)
+        return pltpu.make_async_copy(x_hbm.at[rows], x_ref.at[rows], sems.at[step])
+
+    copy(0).start()
+    keeps = pltpu.make_async_copy(keep_hbm, keep_ref, sems.at[steps])
+    keeps.start()
+    for step in range(1, GRAM_AHEAD):
+        copy(step).start()
+    acc_ref[...] = jnp.zeros_like(acc_ref)
+
+    def add(step, _):
+        @pl.when(step + GRAM_AHEAD < steps)
+        def _():
+            copy(step + GRAM_AHEAD).start()
+
+        copy(step).wait()
+        start = pl.multiple_of(step * GRAM_CELLS, GRAM_CELLS)
+        x = x_ref[pl.ds(start, GRAM_CELLS)]
+        keep = keep_ref[:, pl.ds(start, GRAM_CELLS)]
+        kept = x.T * keep.astype(f32).astype(bf16)
+        by_real = dot(kept, x[:, :half])
+        by_imag = dot(kept[half:], x[:, half:])
+        acc_ref[:half] += by_real[:half] + by_imag
+        acc_ref[half:] += by_real[half:]
+        return 0
+
+    keeps.wait()
+    lax.fori_loop(0, steps, add, 0)
+    real = acc_ref[:half]
+    cross = acc_ref[half:]
+    imag = cross - cross.T
+    rows = lax.broadcasted_iota(jnp.int32, (half, half), 0)
+    cols = lax.broadcasted_iota(jnp.int32, (half, half), 1)
+    packed = jnp.where(rows <= cols, real, imag)
+    trace = jnp.sum(jnp.where(rows == cols, real, 0.0), keepdims=True)
+    parts = half // 8
+    span = out_ref.shape[0] // parts
+    for part in range(parts):
+        lines = packed[8 * part : 8 * part + 8]
+        for block in range(half // LANES):
+            out_ref[span * part + 8 * block : span * part + 8 * block + 8] = lines[
+                :, LANES * block : LANES * block + LANES
+            ]
+        out_ref[span * part + span - 1 : span * part + span] = jnp.broadcast_to(trace, (1, LANES))
 
 
 def local_gram(snaps, keep):
@@ -66,14 +84,15 @@
     span = 8 * half // LANES + 1
     return pl.pallas_call(
         gram_body,
-        grid=(cells // GRAM_CELLS,),
-        in_specs=[
-            pl.BlockSpec((GRAM_CELLS, width), lambda i: (i, 0)),
-            pl.BlockSpec((1, GRAM_CELLS), lambda i: (0, i)),
+        in_specs=[pl.BlockSpec(memory_space=pl.ANY)] * 2,
+        out_specs=pl.BlockSpec(memory_space=pltpu.VMEM),
+        out_shape=jax.ShapeDtypeStruct((half // 8 * span, LANES), f32),
+        scratch_shapes=[
+            pltpu.VMEM((cells, width), bf16),
+            pltpu.VMEM((1, cells), jnp.int32),
+            pltpu.VMEM((width, half), f32),
+            pltpu.SemaphoreType.DMA((cells // GRAM_CELLS + 1,)),
         ],
-        out_specs=pl.BlockSpec((half // 8 * span, LANES), lambda i: (0, 0)),
-        out_shape=jax.ShapeDtypeStruct((half // 8 * span, LANES), f32),
-        scratch_shapes=[pltpu.VMEM((width, half), f32)],
         name="gram",
     )(snaps, keep)
 
@@ -87,8 +106,17 @@
     return dot(jnp.concatenate([ah, ah, al], 1), jnp.concatenate([bh, bl, bh], 0))
 
 
-def solve_body(gathered_ref, power_ref, sr_ref, si_ref, out_ref, ar, ai, er, ei, xr, xi):
+def solve_body(
+    gathered_ref, power_ref, sr_ref, si_ref, x_hbm, out_hbm, x_ref, out_ref, ar, ai, er, ei, xr, xi, sems
+):
     n = ar.shape[0]
+    cells = x_ref.shape[0]
+    chunks = cells // FILTER_CELLS
+    spans = [pl.ds(FILTER_CELLS * i, FILTER_CELLS) for i in range(chunks)]
+    arrivals = [
+        pltpu.make_async_copy(x_hbm.at[span], x_ref.at[span], sems.at[0, i])
+        for i, span in enumerate(spans)
+    ]
     lines = gathered_ref[...].reshape(n // 8, n // LANES, 8, LANES)
     p = jnp.concatenate([lines[:, b].reshape(n, LANES) for b in range(n // LANES)], 1)
     rows = lax.broadcasted_iota(jnp.int32, (n, n), 0)
@@ -105,10 +133,22 @@
     full = jnp.where(eye, re + low, re)
     ar[...] = full
     ai[...] = im
-    er[...] = jnp.where(eye, 1.0, 0.0) - alpha * full
-    ei[...] = -alpha * im
-    xr[...] = alpha * jnp.where(eye, 1.0, 0.0)
-    xi[...] = jnp.zeros_like(im)
+    e_r = jnp.where(eye, 1.0, 0.0) - alpha * full
+    e_i = -alpha * im
+    (rh, rl), (ih, il) = halves(e_r), halves(e_i)
+    top = jnp.concatenate([rh, ih], 1)
+    rest = jnp.concatenate([rl, il], 1)
+    by_real = three(rh, rl, top, rest)
+    by_imag = three(ih, il, top, rest)
+    mu = 2.0 / (2.0 - rho * rho)
+    er[...] = mu * (by_real[:, :n] - by_imag[:, n:]) + jnp.where(eye, 1.0 - mu, 0.0)
+    ei[...] = mu * (by_real[:, n:] + by_imag[:, :n])
+    xr[...] = (mu * alpha) * (jnp.where(eye, 1.0, 0.0) + e_r)
+    xi[...] = (mu * alpha) * e_i
+    rho = rho * rho * mu * 0.5
+
+    for arrival in arrivals:
+        arrival.start()
 
     def step(exact, rho):
         e_r, e_i, x_r, x_i = er[...], ei[...], xr[...], xi[...]
@@ -131,7 +171,17 @@
         return rho * rho * mu * 0.5
 
     rho = lax.while_loop(lambda r: r > 0.5, functools.partial(step, True), rho)
-    lax.while_loop(lambda r: r > 1e-3, functools.partial(step, False), rho)
+    rho = lax.while_loop(lambda r: r > 0.05, functools.partial(step, False), rho)
+
+    @pl.when(rho > 1e-3)
+    def _():
+        e_r, e_i, x_r, x_i = er[...], ei[...], xr[...], xi[...]
+        both = jnp.concatenate([x_r.astype(bf16), x_i.astype(bf16)], 1)
+        by_real = dot(e_r.astype(bf16), both)
+        by_imag = dot(e_i.astype(bf16), both)
+        xr[...] = x_r + by_real[:, :n] - by_imag[:, n:]
+        xi[...] = x_i + by_real[:, n:] + by_imag[:, :n]
+
     s_r, s_i = sr_ref[...], si_ref[...]
     (xh, xl), (yh, yl) = halves(xr[...]), halves(xi[...])
     top = jnp.concatenate([jnp.concatenate([xh, -yh], 1), jnp.concatenate([yh, xh], 1)], 0)
@@ -151,42 +201,32 @@
     gain = jnp.sum(s_r * w_r + s_i * w_i, axis=1, keepdims=True)
     t_r = (w_r / gain).astype(bf16)
     t_i = (w_i / gain).astype(bf16)
-    m = s_r.shape[0]
-    out_ref[:m, :n] = t_r
-    out_ref[:m, n:] = t_i
-    out_ref[m:, :n] = -t_i
-    out_ref[m:, n:] = t_r
-
-
-def solve(gathered, noise, steer_real, steer_imag):
+    taps = jnp.concatenate([jnp.concatenate([t_r, t_i], 1), jnp.concatenate([-t_i, t_r], 1)], 0)
+    leaving = []
+    for i, span in enumerate(spans):
+        arrivals[i].wait()
+        out_ref[:, span] = lax.dot_general(
+            taps, x_ref[span], (((1,), (1,)), ((), ())), preferred_element_type=f32
+        ).astype(bf16)
+        leaving.append(pltpu.make_async_copy(out_ref.at[:, span], out_hbm.at[:, span], sems.at[1, i]))
+        leaving[i].start()
+    for copy in leaving:
+        copy.wait()
+
+
+def solve_and_filter(gathered, noise, steer_real, steer_imag, snaps):
     m, n = steer_real.shape
+    cells, width = snaps.shape
     return pl.pallas_call(
         solve_body,
-        out_shape=jax.ShapeDtypeStruct((2 * m, 2 * n), bf16),
-        scratch_shapes=[pltpu.VMEM((n, n), f32)] * 6,
+        in_specs=[pl.BlockSpec(memory_space=pltpu.VMEM)] * 4 + [pl.BlockSpec(memory_space=pl.ANY)],
+        out_specs=pl.BlockSpec(memory_space=pl.ANY),
+        out_shape=jax.ShapeDtypeStruct((2 * m, cells), bf16),
+        scratch_shapes=[pltpu.VMEM((cells, width), bf16), pltpu.VMEM((2 * m, cells), bf16)]
+        + [pltpu.VMEM((n, n), f32)] * 6
+        + [pltpu.SemaphoreType.DMA((2, cells // FILTER_CELLS))],
         name="solve",
-    )(gathered, noise, steer_real, steer_imag)
-
-
-def filter_body(taps_ref, x_ref, out_ref):
-    out_ref[...] = lax.dot_general(
-        taps_ref[...], x_ref[...], (((1,), (1,)), ((), ())), preferred_element_type=f32
-    ).astype(bf16)
-
-
-def filtered(taps, snaps):
-    cells, width = snaps.shape
-    return pl.pallas_call(
-        filter_body,
-        grid=(cells // FILTER_CELLS,),
-        in_specs=[
-            pl.BlockSpec(taps.shape, lambda i: (0, 0)),
-            pl.BlockSpec((FILTER_CELLS, width), lambda i: (i, 0)),
-        ],
-        out_specs=pl.BlockSpec((taps.shape[0], FILTER_CELLS), lambda i: (0, i)),
-        out_shape=jax.ShapeDtypeStruct((taps.shape[0], cells), bf16),
-        name="filter",
-    )(taps, snaps)
+    )(gathered, noise, steer_real, steer_imag, snaps)
 
 
 def steering(doppler, chans, pulses):
@@ -226,8 +266,9 @@
     power = sum_of_few(trace, "bins")
     noise = power / (lax.axis_size("bins") * half)
     steer_real, steer_imag = steering(doppler[0], CHANNELS, PULSES)
-    taps = solve(gathered.reshape(-1, LANES), noise, steer_real, steer_imag)
-    return filtered(taps, snaps)[None]
+    inputs = (gathered.reshape(-1, LANES), noise, steer_real, steer_imag)
+    inputs = [pltpu.with_memory_space_constraint(v, pltpu.VMEM) for v in inputs]
+    return solve_and_filter(*inputs, snaps)[None]
 
 
 def solution(mesh):

time: 70.4 us -> 59.5 us (0.85); the launches traced: 69.3 us -> 59.3 us
  Pallas kernels: 26 us -> 16.7 us
  other arithmetic: 1.97 us -> 0.75 us
  waiting for transfers between devices: 21.4 us -> 22.6 us
    pallas_call x3 -> x2, Pallas kernels: 26 us -> 16.7 us  [the longest x1 10.1 us: solve_and_filter(): pl.pallas_call(solve_body, in_specs=[pl.BlockSpec(memory_space=pltpu.VMEM...]
    ppermute x3, waiting for transfers between devices: 5.15 us -> 5.86 us  [sum_of_few(): x = x + lax.ppermute(x, axis, [(i, i ^ stride) for i in range(size)])]
    div x1, other arithmetic: 1.25 us -> 0.55 us  [steering(): return (jnp.cos(phase) / scale, jnp.sin(phase) / scale)]
  transfers between devices with their start and end apart: 5 -> 5, of which waited for: 4 -> 4; matrix products, arithmetic and copies ran while one was open for 4% -> 2% of each run, Pallas kernels for 0% -> 0%
where the time goes in v1:
time: 59.5 us; the launch traced here: 59.3 us
  waiting for transfers between devices  22.6 us (38%)
  starting transfers between devices  18.4 us (31%)
  Pallas kernels  16.7 us (28%)
  other arithmetic  0.75 us (1%)
  local copies, waits for them, and re-layouts  0.74 us (1%)
    all_to_all x2, waiting for transfers between devices, exchange(): return lax.all_to_all(x, axis, split_axis=0, concat_axis=0, tiled=True)  16.8 us
    all_to_all x2, starting transfers between devices, exchange(): return lax.all_to_all(x, axis, split_axis=0, concat_axis=0, tiled=True)  16 us
    pallas_call x1, Pallas kernels, solve_and_filter(): pl.pallas_call(solve_body, in_specs=[pl.BlockSpec(memory_space=pltpu.VMEM...  10.1 us
    pallas_call x1, Pallas kernels, local_gram(): pl.pallas_call(gram_body, in_specs=[pl.BlockSpec(memory_space=pl.ANY)] *...  6.63 us
    ppermute x3, waiting for transfers between devices, sum_of_few(): x = x + lax.ppermute(x, axis, [(i, i ^ stride) for i in range(size)])  5.86 us
    ppermute x3, starting transfers between devices, sum_of_few(): x = x + lax.ppermute(x, axis, [(i, i ^ stride) for i in range(size)])  2.41 us
  transfers between devices with their start and end apart: 5, of which 4 were waited for; matrix products, arithmetic and copies ran while one was open for 2% of the time, Pallas kernels for 0%

profile of v1, /device:TPU:38, one launch (start us, length us, event | category | flops | bytes accessed | tf_op | source)
XLA Modules:
  0.0 59.3 jit_solution(16006216874081448434)
XLA Ops:
  0.0 0.0 copy-start
  0.0 6.6 %gram.1 = f32[544,128]{1,0:T(8,128)} custom-call(bf16[8192,512]{1,0:T(8,128)(2,1)} %bitcast.9, s32[1,8192]{1,0:T(1,128)} %bitcast.12), custom_call_target="tpu_custom_call" | custom-call | tf_op jit(solution)/shard_map/gram/pallas_call | solution.py:85
  6.6 11.4 %all-to-all-start = ((f32[32,1,2176]{2,1,0:T(1,128)}), f32[32,1,2176]{2,1,0:T(1,128)S(1)}, u32[]{:S(2)}, u32[]{:S(2)}) async-start(f32[32,1,2176]{2,1,0:T(1,128)} %bitcast.11), calls=%async_computation | async-start | bytes 557056 | tf_op jit(solution)/shard_map/all_to_all | solution.py:243
  18.0 0.0 copy-done
  18.0 12.6 %all-to-all-done = f32[32,1,2176]{2,1,0:T(1,128)S(1)} async-done(((f32[32,1,2176]{2,1,0:T(1,128)}), f32[32,1,2176]{2,1,0:T(1,128)S(1)}, u32[]{:S(2)}, u32[]{:S(2)}) %all-to-all-start) | async-done | bytes 278560 | tf_op jit(solution)/shard_map/all_to_all | solution.py:243
  30.6 0.2 reduce_sum.11
  30.8 0.1 collective-permute-start
  31.0 0.7 %broadcast_in_dim.4 = f32[32,16,128]{2,1,0:T(8,128)} broadcast(f32[16,128]{1,0:T(8,128)S(1)} %bitcast.13), dimensions={1,2} | broadcast | bytes 270336 | tf_op jit(solution)/shard_map/broadcast_in_dim | solution.py:265
  31.7 4.6 %all-to-all-start.1 = ((f32[32,16,128]{2,1,0:T(8,128)}), f32[32,16,128]{2,1,0:T(8,128)S(1)}, u32[]{:S(2)}, u32[]{:S(2)}) async-start(f32[32,16,128]{2,1,0:T(8,128)} %broadcast_in_dim.4), calls=%async_computation.1 | async-start | bytes 524288 | tf_op jit(solution)/shard_map/all_to_all | solution.py:243
  36.3 0.0 collective-permute-done
  36.3 0.9 %collective-permute-start.1 = (f32[1,128]{1,0:T(1,128)S(1)}, f32[1,128]{1,0:T(1,128)S(1)}, u32[]{:S(2)}, u32[]{:S(2)}) collective-permute-start(f32[1,128]{1,0:T(1,128)S(1)} %slice_add_fusion), channel_id=1, source_target_pairs={{0,2},{1,3},{2,0},{3,1},{4,6},{5,7},{6,4},{7,5},{8,10},{9,11},{10,... | collective-permute-start | bytes 1544 | tf_op jit(solution)/shard_map/ppermute | solution.py:250
  37.2 2.7 %collective-permute-done.1 = f32[1,128]{1,0:T(1,128)S(1)} collective-permute-done((f32[1,128]{1,0:T(1,128)S(1)}, f32[1,128]{1,0:T(1,128)S(1)}, u32[]{:S(2)}, u32[]{:S(2)}) %collective-permute-start.1) | collective-permute-done | bytes 544 | tf_op jit(solution)/shard_map/ppermute | solution.py:250
  40.0 1.4 %collective-permute-start.2 = (f32[1,128]{1,0:T(1,128)S(1)}, f32[1,128]{1,0:T(1,128)S(1)}, u32[]{:S(2)}, u32[]{:S(2)}) collective-permute-start(f32[1,128]{1,0:T(1,128)S(1)} %add.39), channel_id=1, source_target_pairs={{0,4},{1,5},{2,6},{3,7},{4,0},{5,1},{6,2},{7,3},{8,12},{9,13},{10,... | collective-permute-start | bytes 1544 | tf_op jit(solution)/shard_map/ppermute | solution.py:250
  41.4 0.5 sine_multiply_fusion
  41.9 3.1 %collective-permute-done.2 = f32[1,128]{1,0:T(1,128)S(1)} collective-permute-done((f32[1,128]{1,0:T(1,128)S(1)}, f32[1,128]{1,0:T(1,128)S(1)}, u32[]{:S(2)}, u32[]{:S(2)}) %collective-permute-start.2) | collective-permute-done | bytes 544 | tf_op jit(solution)/shard_map/ppermute | solution.py:250
  45.0 4.2 %all-to-all-done.1 = f32[32,16,128]{2,1,0:T(8,128)S(1)} async-done(((f32[32,16,128]{2,1,0:T(8,128)}), f32[32,16,128]{2,1,0:T(8,128)S(1)}, u32[]{:S(2)}, u32[]{:S(2)}) %all-to-all-start.1) | async-done | bytes 262176 | tf_op jit(solution)/shard_map/all_to_all | solution.py:243
  49.2 10.1 %solve.1 = bf16[256,8192]{1,0:T(8,128)(2,1)} custom-call(f32[512,128]{1,0:T(8,128)S(1)} %bitcast.8, f32[1,128]{1,0:T(1,128)S(1)} %add_multiply_fusion.1.power_ref, f32[128,256]{1,0:T(8,128)S(1)} %get-tuple-element.6.sr_ref, f32[128,256]{1,0:T(8,128)S(1)} %get-tuple-element.5.si_ref, bf16[8192,512]{1,0:T(8,128)(2,1)} %bitcast.10), custom_call_target="tpu_custom_call" | custom-call | tf_op jit(solution)/shard_map/solve/pallas_call | solution.py:220
  (9 shorter events, 0.0 us)
Async XLA Ops:
  0.0 18.0 %copy-start = (s32[1,128]{1,0:T(1,128)S(1)}, s32[1,128]{1,0:T(1,128)}, u32[]{:S(2)}) copy-start(s32[1,128]{1,0:T(1,128)} %param.5) | copy-start | bytes 1540
  6.6 24.0 %all-to-all-start = ((f32[32,1,2176]{2,1,0:T(1,128)}), f32[32,1,2176]{2,1,0:T(1,128)S(1)}, u32[]{:S(2)}, u32[]{:S(2)}) async-start(f32[32,1,2176]{2,1,0:T(1,128)} %bitcast.11), calls=%async_computation | async-start | bytes 557056 | tf_op jit(solution)/shard_map/all_to_all | solution.py:243
  30.8 5.4 %collective-permute-start = (f32[1,128]{1,0:T(1,128)S(1)}, f32[1,128]{1,0:T(1,128)S(1)}, u32[]{:S(2)}, u32[]{:S(2)}) collective-permute-start(f32[1,128]{1,0:T(1,128)S(1)} %slice.9), channel_id=1, source_target_pairs={{0,1},{1,0},{2,3},{3,2},{4,5},{5,4},{6,7},{7,6},{8,9},{9,8},{10,11... | collective-permute-start | bytes 1544 | tf_op jit(solution)/shard_map/ppermute | solution.py:250
  31.7 17.5 %all-to-all-start.1 = ((f32[32,16,128]{2,1,0:T(8,128)}), f32[32,16,128]{2,1,0:T(8,128)S(1)}, u32[]{:S(2)}, u32[]{:S(2)}) async-start(f32[32,16,128]{2,1,0:T(8,128)} %broadcast_in_dim.4), calls=%async_computation.1 | async-start | bytes 524288 | tf_op jit(solution)/shard_map/all_to_all | solution.py:243
  36.3 3.7 %collective-permute-start.1 = (f32[1,128]{1,0:T(1,128)S(1)}, f32[1,128]{1,0:T(1,128)S(1)}, u32[]{:S(2)}, u32[]{:S(2)}) collective-permute-start(f32[1,128]{1,0:T(1,128)S(1)} %slice_add_fusion), channel_id=1, source_target_pairs={{0,2},{1,3},{2,0},{3,1},{4,6},{5,7},{6,4},{7,5},{8,10},{9,11},{10,... | collective-permute-start | bytes 1544 | tf_op jit(solution)/shard_map/ppermute | solution.py:250
  40.0 5.1 %collective-permute-start.2 = (f32[1,128]{1,0:T(1,128)S(1)}, f32[1,128]{1,0:T(1,128)S(1)}, u32[]{:S(2)}, u32[]{:S(2)}) collective-permute-start(f32[1,128]{1,0:T(1,128)S(1)} %add.39), channel_id=1, source_target_pairs={{0,4},{1,5},{2,6},{3,7},{4,0},{5,1},{6,2},{7,3},{8,12},{9,13},{10,... | collective-permute-start | bytes 1544 | tf_op jit(solution)/shard_map/ppermute | solution.py:250

commit v2 on v1

--- a/solution.py
+++ b/solution.py
@@ -13,7 +13,7 @@
 LANES = 128
 GRAM_CELLS = 2048
 GRAM_AHEAD = 4
-FILTER_CELLS = 2048
+FILTER_CELLS = 1024
 
 load_ratio = 0.5
 look_freq = 0.125
@@ -113,10 +113,7 @@
     cells = x_ref.shape[0]
     chunks = cells // FILTER_CELLS
     spans = [pl.ds(FILTER_CELLS * i, FILTER_CELLS) for i in range(chunks)]
-    arrivals = [
-        pltpu.make_async_copy(x_hbm.at[span], x_ref.at[span], sems.at[0, i])
-        for i, span in enumerate(spans)
-    ]
+    arrival = pltpu.make_async_copy(x_hbm, x_ref, sems.at[0])
     lines = gathered_ref[...].reshape(n // 8, n // LANES, 8, LANES)
     p = jnp.concatenate([lines[:, b].reshape(n, LANES) for b in range(n // LANES)], 1)
     rows = lax.broadcasted_iota(jnp.int32, (n, n), 0)
@@ -135,39 +132,43 @@
     ai[...] = im
     e_r = jnp.where(eye, 1.0, 0.0) - alpha * full
     e_i = -alpha * im
-    (rh, rl), (ih, il) = halves(e_r), halves(e_i)
-    top = jnp.concatenate([rh, ih], 1)
-    rest = jnp.concatenate([rl, il], 1)
-    by_real = three(rh, rl, top, rest)
-    by_imag = three(ih, il, top, rest)
+    reals, imags, sums = [three(a, b, a, b) for a, b in map(halves, (e_r, e_i, e_r + e_i))]
     mu = 2.0 / (2.0 - rho * rho)
-    er[...] = mu * (by_real[:, :n] - by_imag[:, n:]) + jnp.where(eye, 1.0 - mu, 0.0)
-    ei[...] = mu * (by_real[:, n:] + by_imag[:, :n])
+    er[...] = mu * (reals - imags) + jnp.where(eye, 1.0 - mu, 0.0)
+    ei[...] = mu * (sums - (reals + imags))
     xr[...] = (mu * alpha) * (jnp.where(eye, 1.0, 0.0) + e_r)
     xi[...] = (mu * alpha) * e_i
     rho = rho * rho * mu * 0.5
 
-    for arrival in arrivals:
-        arrival.start()
+    arrival.start()
 
     def step(exact, rho):
         e_r, e_i, x_r, x_i = er[...], ei[...], xr[...], xi[...]
         if exact:
-            (rh, rl), (ih, il) = halves(e_r), halves(e_i)
-            (xh, xl), (yh, yl) = halves(x_r), halves(x_i)
-            top = jnp.concatenate([rh, ih, xh, yh], 1)
-            rest = jnp.concatenate([rl, il, xl, yl], 1)
-            by_real = three(rh, rl, top, rest)
-            by_imag = three(ih, il, top, rest)
+            (rh, rl), (ih, il), (gh, gl) = halves(e_r), halves(e_i), halves(e_r + e_i)
+            (xh, xl), (yh, yl), (zh, zl) = halves(x_r), halves(x_i), halves(x_r + x_i)
+            operands = [(rh, rl, xh, xl), (ih, il, yh, yl), (gh, gl, zh, zl)]
+            reals, imags, sums = [
+                three(a, b, jnp.concatenate([a, c], 1), jnp.concatenate([b, d], 1))
+                for a, b, c, d in operands
+            ]
+            real_part = reals - imags
+            imag_part = sums - (reals + imags)
         else:
             both = jnp.concatenate([v.astype(bf16) for v in (e_r, e_i, x_r, x_i)], 1)
             by_real = dot(both[:, :n], both)
             by_imag = dot(both[:, n : 2 * n], both)
+            real_part = jnp.concatenate(
+                [by_real[:, :n] - by_imag[:, n : 2 * n], by_real[:, 2 * n : 3 * n] - by_imag[:, 3 * n :]], 1
+            )
+            imag_part = jnp.concatenate(
+                [by_real[:, n : 2 * n] + by_imag[:, :n], by_real[:, 3 * n :] + by_imag[:, 2 * n : 3 * n]], 1
+            )
         mu = 2.0 / (2.0 - rho * rho)
-        er[...] = mu * (by_real[:, :n] - by_imag[:, n : 2 * n]) + jnp.where(eye, 1.0 - mu, 0.0)
-        ei[...] = mu * (by_real[:, n : 2 * n] + by_imag[:, :n])
-        xr[...] = mu * (x_r + by_real[:, 2 * n : 3 * n] - by_imag[:, 3 * n :])
-        xi[...] = mu * (x_i + by_real[:, 3 * n :] + by_imag[:, 2 * n : 3 * n])
+        er[...] = mu * real_part[:, :n] + jnp.where(eye, 1.0 - mu, 0.0)
+        ei[...] = mu * imag_part[:, :n]
+        xr[...] = mu * (x_r + real_part[:, n:])
+        xi[...] = mu * (x_i + imag_part[:, n:])
         return rho * rho * mu * 0.5
 
     rho = lax.while_loop(lambda r: r > 0.5, functools.partial(step, True), rho)
@@ -202,13 +203,13 @@
     t_r = (w_r / gain).astype(bf16)
     t_i = (w_i / gain).astype(bf16)
     taps = jnp.concatenate([jnp.concatenate([t_r, t_i], 1), jnp.concatenate([-t_i, t_r], 1)], 0)
+    arrival.wait()
     leaving = []
     for i, span in enumerate(spans):
-        arrivals[i].wait()
         out_ref[:, span] = lax.dot_general(
             taps, x_ref[span], (((1,), (1,)), ((), ())), preferred_element_type=f32
         ).astype(bf16)
-        leaving.append(pltpu.make_async_copy(out_ref.at[:, span], out_hbm.at[:, span], sems.at[1, i]))
+        leaving.append(pltpu.make_async_copy(out_ref.at[:, span], out_hbm.at[:, span], sems.at[1 + i]))
         leaving[i].start()
     for copy in leaving:
         copy.wait()
@@ -224,7 +225,7 @@
         out_shape=jax.ShapeDtypeStruct((2 * m, cells), bf16),
         scratch_shapes=[pltpu.VMEM((cells, width), bf16), pltpu.VMEM((2 * m, cells), bf16)]
         + [pltpu.VMEM((n, n), f32)] * 6
-        + [pltpu.SemaphoreType.DMA((2, cells // FILTER_CELLS))],
+        + [pltpu.SemaphoreType.DMA((1 + cells // FILTER_CELLS,))],
         name="solve",
     )(gathered, noise, steer_real, steer_imag, snaps)
 

time: 59.5 us -> 57.8 us (0.971)
  Pallas kernels: 16.7 us -> 15 us
    pallas_call x1, Pallas kernels: 10.1 us -> 8.34 us  [solve_and_filter(): pl.pallas_call(solve_body, in_specs=[pl.BlockSpec(memory_space=pltpu.VMEM...]
where the time goes in v2:
time: 57.8 us; the launch traced here: 57.5 us
  waiting for transfers between devices  22.6 us (39%)
  starting transfers between devices  18.4 us (32%)
  Pallas kernels  15 us (26%)
  other arithmetic  0.75 us (1%)
  local copies, waits for them, and re-layouts  0.74 us (1%)
    all_to_all x2, waiting for transfers between devices, exchange(): return lax.all_to_all(x, axis, split_axis=0, concat_axis=0, tiled=True)  16.8 us
    all_to_all x2, starting transfers between devices, exchange(): return lax.all_to_all(x, axis, split_axis=0, concat_axis=0, tiled=True)  16 us
    pallas_call x1, Pallas kernels, solve_and_filter(): pl.pallas_call(solve_body, in_specs=[pl.BlockSpec(memory_space=pltpu.VMEM...  8.34 us
    pallas_call x1, Pallas kernels, local_gram(): pl.pallas_call(gram_body, in_specs=[pl.BlockSpec(memory_space=pl.ANY)] *...  6.63 us
    ppermute x3, waiting for transfers between devices, sum_of_few(): x = x + lax.ppermute(x, axis, [(i, i ^ stride) for i in range(size)])  5.86 us
    ppermute x3, starting transfers between devices, sum_of_few(): x = x + lax.ppermute(x, axis, [(i, i ^ stride) for i in range(size)])  2.41 us
  transfers between devices with their start and end apart: 5, of which 4 were waited for; matrix products, arithmetic and copies ran while one was open for 2% of the time, Pallas kernels for 0%

profile of v2, /device:TPU:38, one launch (start us, length us, event | category | flops | bytes accessed | tf_op | source)
XLA Modules:
  0.0 57.5 jit_solution(5834401203995535841)
XLA Ops:
  0.0 0.0 copy-start
  0.0 6.6 %gram.1 = f32[544,128]{1,0:T(8,128)} custom-call(bf16[8192,512]{1,0:T(8,128)(2,1)} %bitcast.9, s32[1,8192]{1,0:T(1,128)} %bitcast.12), custom_call_target="tpu_custom_call" | custom-call | tf_op jit(solution)/shard_map/gram/pallas_call | solution.py:85
  6.6 11.4 %all-to-all-start = ((f32[32,1,2176]{2,1,0:T(1,128)}), f32[32,1,2176]{2,1,0:T(1,128)S(1)}, u32[]{:S(2)}, u32[]{:S(2)}) async-start(f32[32,1,2176]{2,1,0:T(1,128)} %bitcast.11), calls=%async_computation | async-start | bytes 557056 | tf_op jit(solution)/shard_map/all_to_all | solution.py:244
  18.0 0.0 copy-done
  18.0 12.6 %all-to-all-done = f32[32,1,2176]{2,1,0:T(1,128)S(1)} async-done(((f32[32,1,2176]{2,1,0:T(1,128)}), f32[32,1,2176]{2,1,0:T(1,128)S(1)}, u32[]{:S(2)}, u32[]{:S(2)}) %all-to-all-start) | async-done | bytes 278560 | tf_op jit(solution)/shard_map/all_to_all | solution.py:244
  30.6 0.2 reduce_sum.11
  30.8 0.1 collective-permute-start
  31.0 0.7 %broadcast_in_dim.4 = f32[32,16,128]{2,1,0:T(8,128)} broadcast(f32[16,128]{1,0:T(8,128)S(1)} %bitcast.13), dimensions={1,2} | broadcast | bytes 270336 | tf_op jit(solution)/shard_map/broadcast_in_dim | solution.py:266
  31.7 4.6 %all-to-all-start.1 = ((f32[32,16,128]{2,1,0:T(8,128)}), f32[32,16,128]{2,1,0:T(8,128)S(1)}, u32[]{:S(2)}, u32[]{:S(2)}) async-start(f32[32,16,128]{2,1,0:T(8,128)} %broadcast_in_dim.4), calls=%async_computation.1 | async-start | bytes 524288 | tf_op jit(solution)/shard_map/all_to_all | solution.py:244
  36.3 0.0 collective-permute-done
  36.3 0.9 %collective-permute-start.1 = (f32[1,128]{1,0:T(1,128)S(1)}, f32[1,128]{1,0:T(1,128)S(1)}, u32[]{:S(2)}, u32[]{:S(2)}) collective-permute-start(f32[1,128]{1,0:T(1,128)S(1)} %slice_add_fusion), channel_id=1, source_target_pairs={{0,2},{1,3},{2,0},{3,1},{4,6},{5,7},{6,4},{7,5},{8,10},{9,11},{10,... | collective-permute-start | bytes 1544 | tf_op jit(solution)/shard_map/ppermute | solution.py:251
  37.2 2.7 %collective-permute-done.1 = f32[1,128]{1,0:T(1,128)S(1)} collective-permute-done((f32[1,128]{1,0:T(1,128)S(1)}, f32[1,128]{1,0:T(1,128)S(1)}, u32[]{:S(2)}, u32[]{:S(2)}) %collective-permute-start.1) | collective-permute-done | bytes 544 | tf_op jit(solution)/shard_map/ppermute | solution.py:251
  40.0 1.4 %collective-permute-start.2 = (f32[1,128]{1,0:T(1,128)S(1)}, f32[1,128]{1,0:T(1,128)S(1)}, u32[]{:S(2)}, u32[]{:S(2)}) collective-permute-start(f32[1,128]{1,0:T(1,128)S(1)} %add.39), channel_id=1, source_target_pairs={{0,4},{1,5},{2,6},{3,7},{4,0},{5,1},{6,2},{7,3},{8,12},{9,13},{10,... | collective-permute-start | bytes 1544 | tf_op jit(solution)/shard_map/ppermute | solution.py:251
  41.4 0.5 sine_multiply_fusion
  41.9 3.1 %collective-permute-done.2 = f32[1,128]{1,0:T(1,128)S(1)} collective-permute-done((f32[1,128]{1,0:T(1,128)S(1)}, f32[1,128]{1,0:T(1,128)S(1)}, u32[]{:S(2)}, u32[]{:S(2)}) %collective-permute-start.2) | collective-permute-done | bytes 544 | tf_op jit(solution)/shard_map/ppermute | solution.py:251
  45.0 4.2 %all-to-all-done.1 = f32[32,16,128]{2,1,0:T(8,128)S(1)} async-done(((f32[32,16,128]{2,1,0:T(8,128)}), f32[32,16,128]{2,1,0:T(8,128)S(1)}, u32[]{:S(2)}, u32[]{:S(2)}) %all-to-all-start.1) | async-done | bytes 262176 | tf_op jit(solution)/shard_map/all_to_all | solution.py:244
  49.2 8.3 %solve.1 = bf16[256,8192]{1,0:T(8,128)(2,1)} custom-call(f32[512,128]{1,0:T(8,128)S(1)} %bitcast.8, f32[1,128]{1,0:T(1,128)S(1)} %add_multiply_fusion.1.power_ref, f32[128,256]{1,0:T(8,128)S(1)} %get-tuple-element.6.sr_ref, f32[128,256]{1,0:T(8,128)S(1)} %get-tuple-element.5.si_ref, bf16[8192,512]{1,0:T(8,128)(2,1)} %bitcast.10), custom_call_target="tpu_custom_call" | custom-call | tf_op jit(solution)/shard_map/solve/pallas_call | solution.py:221
  (9 shorter events, 0.0 us)
Async XLA Ops:
  0.0 18.0 %copy-start = (s32[1,128]{1,0:T(1,128)S(1)}, s32[1,128]{1,0:T(1,128)}, u32[]{:S(2)}) copy-start(s32[1,128]{1,0:T(1,128)} %param.5) | copy-start | bytes 1540
  6.6 24.0 %all-to-all-start = ((f32[32,1,2176]{2,1,0:T(1,128)}), f32[32,1,2176]{2,1,0:T(1,128)S(1)}, u32[]{:S(2)}, u32[]{:S(2)}) async-start(f32[32,1,2176]{2,1,0:T(1,128)} %bitcast.11), calls=%async_computation | async-start | bytes 557056 | tf_op jit(solution)/shard_map/all_to_all | solution.py:244
  30.8 5.4 %collective-permute-start = (f32[1,128]{1,0:T(1,128)S(1)}, f32[1,128]{1,0:T(1,128)S(1)}, u32[]{:S(2)}, u32[]{:S(2)}) collective-permute-start(f32[1,128]{1,0:T(1,128)S(1)} %slice.9), channel_id=1, source_target_pairs={{0,1},{1,0},{2,3},{3,2},{4,5},{5,4},{6,7},{7,6},{8,9},{9,8},{10,11... | collective-permute-start | bytes 1544 | tf_op jit(solution)/shard_map/ppermute | solution.py:251
  31.7 17.5 %all-to-all-start.1 = ((f32[32,16,128]{2,1,0:T(8,128)}), f32[32,16,128]{2,1,0:T(8,128)S(1)}, u32[]{:S(2)}, u32[]{:S(2)}) async-start(f32[32,16,128]{2,1,0:T(8,128)} %broadcast_in_dim.4), calls=%async_computation.1 | async-start | bytes 524288 | tf_op jit(solution)/shard_map/all_to_all | solution.py:244
  36.3 3.7 %collective-permute-start.1 = (f32[1,128]{1,0:T(1,128)S(1)}, f32[1,128]{1,0:T(1,128)S(1)}, u32[]{:S(2)}, u32[]{:S(2)}) collective-permute-start(f32[1,128]{1,0:T(1,128)S(1)} %slice_add_fusion), channel_id=1, source_target_pairs={{0,2},{1,3},{2,0},{3,1},{4,6},{5,7},{6,4},{7,5},{8,10},{9,11},{10,... | collective-permute-start | bytes 1544 | tf_op jit(solution)/shard_map/ppermute | solution.py:251
  40.0 5.1 %collective-permute-start.2 = (f32[1,128]{1,0:T(1,128)S(1)}, f32[1,128]{1,0:T(1,128)S(1)}, u32[]{:S(2)}, u32[]{:S(2)}) collective-permute-start(f32[1,128]{1,0:T(1,128)S(1)} %add.39), channel_id=1, source_target_pairs={{0,4},{1,5},{2,6},{3,7},{4,0},{5,1},{6,2},{7,3},{8,12},{9,13},{10,... | collective-permute-start | bytes 1544 | tf_op jit(solution)/shard_map/ppermute | solution.py:251

commit v3 on v2

--- a/solution.py
+++ b/solution.py
@@ -6,6 +6,7 @@
 from jax.experimental import pallas as pl
 from jax.experimental.pallas import tpu as pltpu
 from jax.sharding import PartitionSpec as P
+
 
 CHANNELS = 16
 PULSES = 16
@@ -126,7 +127,7 @@
     low = load_ratio * power_ref[0:1, 0:1]
     high = jnp.sqrt(jnp.sum(squares, keepdims=True)) + low
     alpha = 2.0 / (low + high)
-    rho = ((high - low) / (high + low))[0, 0]
+    rho = spread = ((high - low) / (high + low))[0, 0]
     full = jnp.where(eye, re + low, re)
     ar[...] = full
     ai[...] = im
@@ -192,13 +193,25 @@
         (rh, rl), (ih, il) = halves(v_r), halves(v_i)
         return three(jnp.concatenate([rh, ih], 1), jnp.concatenate([rl, il], 1), top, rest)
 
-    w = applied(s_r, s_i)
-    a = jnp.concatenate(
-        [jnp.concatenate([ar[...], -ai[...]], 1), jnp.concatenate([ai[...], ar[...]], 1)], 0
-    )
-    back = jnp.dot(w, a, precision=lax.Precision.HIGHEST, preferred_element_type=f32)
-    w = w + applied(s_r - back[:, :n], s_i - back[:, n:])
-    w_r, w_i = w[:, :n], w[:, n:]
+    def corrected(w):
+        a = jnp.concatenate(
+            [jnp.concatenate([ar[...], -ai[...]], 1), jnp.concatenate([ai[...], ar[...]], 1)], 0
+        )
+        back = jnp.dot(w, a, precision=lax.Precision.HIGHEST, preferred_element_type=f32)
+        return w + applied(s_r - back[:, :n], s_i - back[:, n:])
+
+    m = s_r.shape[0]
+    w = corrected(applied(s_r, s_i))
+    er[:m] = w[:, :n]
+    er[m:] = w[:, n:]
+
+    @pl.when(spread > 0.995)
+    def _():
+        w = corrected(jnp.concatenate([er[:m], er[m:]], 1))
+        er[:m] = w[:, :n]
+        er[m:] = w[:, n:]
+
+    w_r, w_i = er[:m], er[m:]
     gain = jnp.sum(s_r * w_r + s_i * w_i, axis=1, keepdims=True)
     t_r = (w_r / gain).astype(bf16)
     t_i = (w_i / gain).astype(bf16)

time: 57.8 us -> 58.2 us (level)
  no operation moved by 1% of the time
where the time goes in v3:
time: 58.2 us; the launch traced here: 57.9 us
  waiting for transfers between devices  22.6 us (39%)
  starting transfers between devices  18.4 us (32%)
  Pallas kernels  15.4 us (26%)
  other arithmetic  0.75 us (1%)
  local copies, waits for them, and re-layouts  0.74 us (1%)
    all_to_all x2, waiting for transfers between devices, exchange(): return lax.all_to_all(x, axis, split_axis=0, concat_axis=0, tiled=True)  16.8 us
    all_to_all x2, starting transfers between devices, exchange(): return lax.all_to_all(x, axis, split_axis=0, concat_axis=0, tiled=True)  16 us
    pallas_call x1, Pallas kernels, solve_and_filter(): pl.pallas_call(solve_body, in_specs=[pl.BlockSpec(memory_space=pltpu.VMEM...  8.74 us
    pallas_call x1, Pallas kernels, local_gram(): pl.pallas_call(gram_body, in_specs=[pl.BlockSpec(memory_space=pl.ANY)] *...  6.63 us
    ppermute x3, waiting for transfers between devices, sum_of_few(): x = x + lax.ppermute(x, axis, [(i, i ^ stride) for i in range(size)])  5.86 us
    ppermute x3, starting transfers between devices, sum_of_few(): x = x + lax.ppermute(x, axis, [(i, i ^ stride) for i in range(size)])  2.41 us
  transfers between devices with their start and end apart: 5, of which 4 were waited for; matrix products, arithmetic and copies ran while one was open for 2% of the time, Pallas kernels for 0%

profile of v3, /device:TPU:38, one launch (start us, length us, event | category | flops | bytes accessed | tf_op | source)
XLA Modules:
  0.0 57.9 jit_solution(7690716162434202368)
XLA Ops:
  0.0 0.0 copy-start
  0.0 6.6 %gram.1 = f32[544,128]{1,0:T(8,128)} custom-call(bf16[8192,512]{1,0:T(8,128)(2,1)} %bitcast.9, s32[1,8192]{1,0:T(1,128)} %bitcast.12), custom_call_target="tpu_custom_call" | custom-call | tf_op jit(solution)/shard_map/gram/pallas_call | solution.py:86
  6.6 11.4 %all-to-all-start = ((f32[32,1,2176]{2,1,0:T(1,128)}), f32[32,1,2176]{2,1,0:T(1,128)S(1)}, u32[]{:S(2)}, u32[]{:S(2)}) async-start(f32[32,1,2176]{2,1,0:T(1,128)} %bitcast.11), calls=%async_computation | async-start | bytes 557056 | tf_op jit(solution)/shard_map/all_to_all | solution.py:257
  18.0 0.0 copy-done
  18.0 12.6 %all-to-all-done = f32[32,1,2176]{2,1,0:T(1,128)S(1)} async-done(((f32[32,1,2176]{2,1,0:T(1,128)}), f32[32,1,2176]{2,1,0:T(1,128)S(1)}, u32[]{:S(2)}, u32[]{:S(2)}) %all-to-all-start) | async-done | bytes 278560 | tf_op jit(solution)/shard_map/all_to_all | solution.py:257
  30.6 0.2 reduce_sum.11
  30.8 0.1 collective-permute-start
  31.0 0.7 %broadcast_in_dim.4 = f32[32,16,128]{2,1,0:T(8,128)} broadcast(f32[16,128]{1,0:T(8,128)S(1)} %bitcast.13), dimensions={1,2} | broadcast | bytes 270336 | tf_op jit(solution)/shard_map/broadcast_in_dim | solution.py:279
  31.7 4.6 %all-to-all-start.1 = ((f32[32,16,128]{2,1,0:T(8,128)}), f32[32,16,128]{2,1,0:T(8,128)S(1)}, u32[]{:S(2)}, u32[]{:S(2)}) async-start(f32[32,16,128]{2,1,0:T(8,128)} %broadcast_in_dim.4), calls=%async_computation.1 | async-start | bytes 524288 | tf_op jit(solution)/shard_map/all_to_all | solution.py:257
  36.3 0.0 collective-permute-done
  36.3 0.9 %collective-permute-start.1 = (f32[1,128]{1,0:T(1,128)S(1)}, f32[1,128]{1,0:T(1,128)S(1)}, u32[]{:S(2)}, u32[]{:S(2)}) collective-permute-start(f32[1,128]{1,0:T(1,128)S(1)} %slice_add_fusion), channel_id=1, source_target_pairs={{0,2},{1,3},{2,0},{3,1},{4,6},{5,7},{6,4},{7,5},{8,10},{9,11},{10,... | collective-permute-start | bytes 1544 | tf_op jit(solution)/shard_map/ppermute | solution.py:264
  37.2 2.7 %collective-permute-done.1 = f32[1,128]{1,0:T(1,128)S(1)} collective-permute-done((f32[1,128]{1,0:T(1,128)S(1)}, f32[1,128]{1,0:T(1,128)S(1)}, u32[]{:S(2)}, u32[]{:S(2)}) %collective-permute-start.1) | collective-permute-done | bytes 544 | tf_op jit(solution)/shard_map/ppermute | solution.py:264
  40.0 1.4 %collective-permute-start.2 = (f32[1,128]{1,0:T(1,128)S(1)}, f32[1,128]{1,0:T(1,128)S(1)}, u32[]{:S(2)}, u32[]{:S(2)}) collective-permute-start(f32[1,128]{1,0:T(1,128)S(1)} %add.39), channel_id=1, source_target_pairs={{0,4},{1,5},{2,6},{3,7},{4,0},{5,1},{6,2},{7,3},{8,12},{9,13},{10,... | collective-permute-start | bytes 1544 | tf_op jit(solution)/shard_map/ppermute | solution.py:264
  41.4 0.5 sine_multiply_fusion
  41.9 3.1 %collective-permute-done.2 = f32[1,128]{1,0:T(1,128)S(1)} collective-permute-done((f32[1,128]{1,0:T(1,128)S(1)}, f32[1,128]{1,0:T(1,128)S(1)}, u32[]{:S(2)}, u32[]{:S(2)}) %collective-permute-start.2) | collective-permute-done | bytes 544 | tf_op jit(solution)/shard_map/ppermute | solution.py:264
  45.0 4.2 %all-to-all-done.1 = f32[32,16,128]{2,1,0:T(8,128)S(1)} async-done(((f32[32,16,128]{2,1,0:T(8,128)}), f32[32,16,128]{2,1,0:T(8,128)S(1)}, u32[]{:S(2)}, u32[]{:S(2)}) %all-to-all-start.1) | async-done | bytes 262176 | tf_op jit(solution)/shard_map/all_to_all | solution.py:257
  49.2 8.7 %solve.1 = bf16[256,8192]{1,0:T(8,128)(2,1)} custom-call(f32[512,128]{1,0:T(8,128)S(1)} %bitcast.8, f32[1,128]{1,0:T(1,128)S(1)} %add_multiply_fusion.1.power_ref, f32[128,256]{1,0:T(8,128)S(1)} %get-tuple-element.6.sr_ref, f32[128,256]{1,0:T(8,128)S(1)} %get-tuple-element.5.si_ref, bf16[8192,512]{1,0:T(8,128)(2,1)} %bitcast.10), custom_call_target="tpu_custom_call" | custom-call | tf_op jit(solution)/shard_map/solve/pallas_call | solution.py:234
  (9 shorter events, 0.0 us)
Async XLA Ops:
  0.0 18.0 %copy-start = (s32[1,128]{1,0:T(1,128)S(1)}, s32[1,128]{1,0:T(1,128)}, u32[]{:S(2)}) copy-start(s32[1,128]{1,0:T(1,128)} %param.5) | copy-start | bytes 1540
  6.6 24.0 %all-to-all-start = ((f32[32,1,2176]{2,1,0:T(1,128)}), f32[32,1,2176]{2,1,0:T(1,128)S(1)}, u32[]{:S(2)}, u32[]{:S(2)}) async-start(f32[32,1,2176]{2,1,0:T(1,128)} %bitcast.11), calls=%async_computation | async-start | bytes 557056 | tf_op jit(solution)/shard_map/all_to_all | solution.py:257
  30.8 5.4 %collective-permute-start = (f32[1,128]{1,0:T(1,128)S(1)}, f32[1,128]{1,0:T(1,128)S(1)}, u32[]{:S(2)}, u32[]{:S(2)}) collective-permute-start(f32[1,128]{1,0:T(1,128)S(1)} %slice.9), channel_id=1, source_target_pairs={{0,1},{1,0},{2,3},{3,2},{4,5},{5,4},{6,7},{7,6},{8,9},{9,8},{10,11... | collective-permute-start | bytes 1544 | tf_op jit(solution)/shard_map/ppermute | solution.py:264
  31.7 17.5 %all-to-all-start.1 = ((f32[32,16,128]{2,1,0:T(8,128)}), f32[32,16,128]{2,1,0:T(8,128)S(1)}, u32[]{:S(2)}, u32[]{:S(2)}) async-start(f32[32,16,128]{2,1,0:T(8,128)} %broadcast_in_dim.4), calls=%async_computation.1 | async-start | bytes 524288 | tf_op jit(solution)/shard_map/all_to_all | solution.py:257
  36.3 3.7 %collective-permute-start.1 = (f32[1,128]{1,0:T(1,128)S(1)}, f32[1,128]{1,0:T(1,128)S(1)}, u32[]{:S(2)}, u32[]{:S(2)}) collective-permute-start(f32[1,128]{1,0:T(1,128)S(1)} %slice_add_fusion), channel_id=1, source_target_pairs={{0,2},{1,3},{2,0},{3,1},{4,6},{5,7},{6,4},{7,5},{8,10},{9,11},{10,... | collective-permute-start | bytes 1544 | tf_op jit(solution)/shard_map/ppermute | solution.py:264
  40.0 5.1 %collective-permute-start.2 = (f32[1,128]{1,0:T(1,128)S(1)}, f32[1,128]{1,0:T(1,128)S(1)}, u32[]{:S(2)}, u32[]{:S(2)}) collective-permute-start(f32[1,128]{1,0:T(1,128)S(1)} %add.39), channel_id=1, source_target_pairs={{0,4},{1,5},{2,6},{3,7},{4,0},{5,1},{6,2},{7,3},{8,12},{9,13},{10,... | collective-permute-start | bytes 1544 | tf_op jit(solution)/shard_map/ppermute | solution.py:264
